TPU v7x, 32 devices: a whole 2x2x4 slice. The times are simulated.
32 devices in a mesh: gx: 4 (over z), gy: 4 (over x, core), gz: 2 (over y).
Axes of the slice: x: 2, y: 2, z: 4, core: 2. Of those that a mesh axis runs over, the one named last changes fastest.
Arguments:
- hidden_in: bfloat16 [2048, 4096], P(('gx', 'gy'), 'gz'), may hold values from -40 to 40
- norm_gain: float32 [4096], P('gz'), may hold values from 0.25 to 1.75
- normed_grad: bfloat16 [2048, 4096], P(('gx', 'gy'), 'gz'), may hold values from -64 to 64
- key_grad: bfloat16 [2048, 512], P(('gx', 'gy')), may hold values from -6 to 6
- weight_blocks: bfloat16 [16, 2, 520, 128], P(('gx', 'gy'), 'gz'), may hold values from -0.09375 to 0.09375
- block_count: int32 [2, 16], P('gz'), may hold values from 1 to 520, as said below
Outputs:
- hidden_grad: bfloat16 [2048, 4096], P(('gx', 'gy'), 'gz')
- weight_grad: float32 [16, 2, 520, 128], P(('gx', 'gy'), 'gz')
Inputs may be any that keep to these rules, and one draw needn't show every extreme that they name: `block_count`: each row sums to 8192; in each row the owners i * 4 to i * 4 + 3 hold together exactly the blocks i * 2048 to min((i + 1) * 2048, 8192) - 1, and one of them holds exactly 520 blocks.
All inputs are finite; a program needn't handle non-finite values.
Results may differ from a plain program's by a relative error of at most 0.0029.
Values may be sent and summed in bfloat16 or wider, within the bound.
A program may use at most 64 MiB of HBM per device.

v0:
```python
import functools
import jax
import jax.numpy as jnp
from jax import lax
from jax.experimental import pallas as pl
from jax.experimental.pallas import tpu as pltpu
from jax.sharding import PartitionSpec as P

EPS = 1e-06
LANE = 128
MESH = pl.DeviceIdType.MESH
VMEM_BUDGET = 48 * 2**20


def owner_windows(outer, inner, blocks, most, per_row, rows):
    group = -(-blocks // outer)
    lows, highs = [], []
    for i in range(outer):
        total = min(group, blocks - i * group)
        for j in range(inner):
            low = max(j, total - (inner - j) * most)
            high = min(min(j * most, total - (inner - j)) + most, total)
            lows.append((i * group + low) // per_row // 8 * 8)
            highs.append(-(-(i * group + high) // per_row))
    height = -(-max(h - l for l, h in zip(lows, highs)) // 16) * 16
    return [min(low, rows - height) for low in lows], height


def fast_kernel(
    dims, windows,
    count_ref, hidden_hbm, gain_ref, ngrad_hbm, key_hbm, wb_hbm,
    hgrad_ref, wgrad_ref,
    hidden_ref, ngrad_ref, wb_ref, kall, nt_send, nt_recv, pt_send, pt_recv, feat, wpad, wflat, wwin, dacc, dflat,
    sq_send, sq_recv, pj_send, pj_recv,
    own_sem, z_send, z_recv, s1_send, s1_recv, s2_send, s2_recv, s3_send, s3_recv,
    n_send, n_recv, p_send, p_recv, e_send, e_recv,
):
    outer, inner, model_width, most, per_row, height, pad = dims
    f32, bf16 = jnp.float32, jnp.bfloat16
    a, b, g = lax.axis_index("gx"), lax.axis_index("gy"), lax.axis_index("gz")
    x, c = b // 2, b % 2
    ox, oc, og = 1 - x, 1 - c, 1 - g
    me = a * inner + b
    tokens, rows = hidden_ref.shape
    owners = outer * inner
    chunks = rows // LANE
    half = tokens // 2

    def peer(rel, k):
        px = ox if k // 2 else x
        pc = oc if k % 2 else c
        return lax.rem(a + rel, outer), px, pc

    def remote(src, dst, send, recv, gx, gy, gz):
        return pltpu.make_async_remote_copy(
            src_ref=src, dst_ref=dst, send_sem=send, recv_sem=recv,
            device_id=(gx, gy, gz), device_id_type=MESH)

    own = [pltpu.make_async_copy(key_hbm.at[pl.ds(h * half, half)], kall.at[a, c, h, x], own_sem.at[h])
           for h in range(2)]
    own += [
        pltpu.make_async_copy(hidden_hbm, hidden_ref, own_sem.at[2]),
        pltpu.make_async_copy(wb_hbm, wb_ref, own_sem.at[3]),
        pltpu.make_async_copy(ngrad_hbm, ngrad_ref, own_sem.at[4]),
    ]
    for copy in own:
        copy.start()

    pairs = [(rel, k) for rel in range(outer) for k in range(inner) if rel or k]
    barrier = pltpu.get_barrier_semaphore()
    for rel, k in pairs:
        pa, px, pc = peer(rel, k)
        pl.semaphore_signal(barrier, inc=1, device_id=(pa, px * 2 + pc, g), device_id_type=MESH)
    pl.semaphore_signal(barrier, inc=1, device_id=(a, b, og), device_id_type=MESH)

    for copy in own[0:2]:
        copy.wait()
    pl.semaphore_wait(barrier, owners)

    sends = []

    def start(copy):
        copy.start()
        sends.append(copy)
        return copy

    zc = {}
    for rel in range(1, outer):
        piece = kall.at[a, c, g, x]
        zc[rel] = start(remote(piece, piece, z_send.at[rel], z_recv.at[rel],
                               lax.rem(a - rel + outer, outer), b, g))
    bx, bc = ox * 2 + c, x * 2 + oc
    own_piece = kall.at[a, c, g, x]
    step1 = {0: start(remote(own_piece, own_piece, s1_send.at[0], s1_recv.at[0], a, bx, g))}
    step2, step3 = {}, {}
    own[2].wait()
    squares = jnp.zeros((tokens, LANE), f32)
    for i in range(chunks):
        part = hidden_ref[:, i * LANE:(i + 1) * LANE].astype(f32)
        squares = squares + part * part
    row_sum = jnp.sum(squares, axis=1, keepdims=True)
    sq_send[...] = jnp.broadcast_to(row_sum, (tokens, LANE)).T[0:8, :]
    sq_copy = start(remote(sq_send, sq_recv, e_send.at[0], e_recv.at[0], a, b, og))

    begin = jnp.int32(0)
    window_low = jnp.int32(0)
    count = jnp.int32(0)
    for o in range(owners):
        value = count_ref[0, o]
        begin = begin + jnp.where(o < me, value, 0)
        count = count + jnp.where(me == o, value, 0)
        window_low = window_low + jnp.where(me == o, windows[o], 0)
    offset = jnp.clip(begin - window_low * per_row, 0, pad)
    flat_rows = height * per_row
    slot = lax.broadcasted_iota(jnp.int32, (most, LANE), 0)
    wpad[...] = jnp.zeros_like(wpad)
    own[3].wait()
    wpad[pad:pad + most, :] = jnp.where(slot < count, wb_ref[...].astype(f32), 0.0)
    wflat[...] = wpad[pl.ds(pad - offset, flat_rows), :]
    for i in range(per_row):
        wwin[:, i * LANE:(i + 1) * LANE] = wflat[pl.ds(i, height, stride=per_row), :].astype(bf16)

    sq_copy.wait_recv()
    total = row_sum + jnp.broadcast_to(sq_recv[0:1, :], (tokens, LANE)).T[:, 0:1]
    rstd = lax.rsqrt(total / model_width + EPS)

    for rel in range(1, outer):
        zc[rel].wait_recv()
        s = lax.rem(a + rel, outer)
        piece = kall.at[s, c, g, x]
        step1[rel] = start(remote(piece, piece, s1_send.at[rel], s1_recv.at[rel], a, bx, g))

    for i in range(chunks):
        cols = slice(i * LANE, (i + 1) * LANE)
        normed = hidden_ref[:, cols].astype(f32) * rstd * gain_ref[:, cols]
        feat[cols, :] = normed.T
    for o in range(owners):
        nt_send[o] = feat[windows[o]:windows[o] + height, :].astype(bf16)
    nc = {}
    for rel, k in pairs:
        pa, px, pc = peer(rel, k)
        nc[rel, k] = start(remote(
            nt_send.at[pa * inner + px * 2 + pc], nt_recv.at[me],
            n_send.at[rel * inner + k], n_recv.at[rel * inner + k], pa, px * 2 + pc, g))

    for rel in range(outer):
        step1[rel].wait_recv()
        s = lax.rem(a + rel, outer)
        piece = kall.at[s, c, g] if rel else kall.at[s, c, g, ox]
        step2[rel] = start(remote(piece, piece, s2_send.at[rel], s2_recv.at[rel], a, b, og))
    for rel in range(outer):
        step2[rel].wait_recv()
        piece = kall.at[lax.rem(a + rel, outer), c]
        step3[rel] = start(remote(piece, piece, s3_send.at[rel], s3_recv.at[rel], a, bc, g))

    def keys(s, px, pc):
        return jnp.concatenate([kall[s, pc, 0, px], kall[s, pc, 1, px]], axis=0)

    pc_copies = {}
    for rel in range(outer):
        step3[rel].wait_recv()
        for k in range(inner):
            pa, px, pc = peer(rel, k)
            to = pa * inner + px * 2 + pc
            product = lax.dot_general(
                wwin[...], keys(pa, px, pc), (((1,), (1,)), ((), ())),
                preferred_element_type=f32).astype(bf16)
            if rel == 0 and k == 0:
                pt_recv[me] = product
            else:
                pt_send[to] = product
                pc_copies[rel, k] = start(remote(
                    pt_send.at[to], pt_recv.at[me],
                    p_send.at[rel * inner + k], p_recv.at[rel * inner + k], pa, px * 2 + pc, g))

    for rel in range(outer):
        for k in range(inner):
            pa, px, pc = peer(outer - rel, k)
            source = pa * inner + px * 2 + pc
            if rel == 0 and k == 0:
                part = nt_send[source]
            else:
                nc[rel, k].wait_recv()
                part = nt_recv[source]
            term = jnp.dot(part, keys(pa, px, pc), preferred_element_type=f32)
            if rel == 0 and k == 0:
                dacc[...] = term
            else:
                dacc[...] += term
    for i in range(per_row):
        dflat[pl.ds(i, height, stride=per_row), :] = dacc[:, i * LANE:(i + 1) * LANE]
    dflat[flat_rows:, :] = jnp.zeros((most, LANE), f32)
    wgrad_ref[...] = jnp.where(slot < count, dflat[pl.ds(offset, most), :], 0.0)

    for rel, k in pairs:
        pc_copies[rel, k].wait_recv()
    own[4].wait()
    feat[...] = jnp.zeros_like(feat)
    for o in range(owners):
        feat[windows[o]:windows[o] + height, :] += pt_recv[o].astype(f32)
    proj = jnp.zeros((tokens, LANE), f32)
    for i in range(chunks):
        cols = slice(i * LANE, (i + 1) * LANE)
        gained = gain_ref[:, cols] * (ngrad_ref[:, cols].astype(f32) + feat[cols, :].T)
        feat[cols, :] = gained
        proj = proj + gained * hidden_ref[:, cols].astype(f32)
    proj_sum = jnp.sum(proj, axis=1, keepdims=True)
    pj_send[...] = jnp.broadcast_to(proj_sum, (tokens, LANE)).T[0:8, :]
    pj_copy = start(remote(pj_send, pj_recv, e_send.at[1], e_recv.at[1], a, b, og))
    pj_copy.wait_recv()
    proj_all = proj_sum + jnp.broadcast_to(pj_recv[0:1, :], (tokens, LANE)).T[:, 0:1]
    scale = rstd * rstd * rstd * proj_all / model_width
    for i in range(chunks):
        cols = slice(i * LANE, (i + 1) * LANE)
        grad = feat[cols, :] * rstd - hidden_ref[:, cols].astype(f32) * scale
        hgrad_ref[:, cols] = grad.astype(bf16)
    for copy in sends:
        copy.wait_send()


def fast_plan(mesh, hidden, key, wb):
    outer, inner, halves = (mesh.shape[n] for n in ("gx", "gy", "gz"))
    tokens, rows, width, most = hidden.shape[0], hidden.shape[1], key.shape[1], wb.shape[2]
    if inner != 4 or halves != 2 or tokens != LANE or rows % LANE or width % LANE or most % 8:
        return None
    per_row = width // LANE
    windows, height = owner_windows(outer, inner, rows * per_row, most, per_row, rows)
    if rows % 16 or min(windows) < 0:
        return None
    held = outer * inner * (tokens * width * 2 + 4 * height * tokens * 2) + 6 * tokens * rows * 4
    if held > VMEM_BUDGET:
        return None
    return windows, height, per_row


def fast_shards(mesh, plan, hidden_in, norm_gain, normed_grad, key_grad, weight_blocks, block_count):
    windows, height, per_row = plan
    outer, inner = mesh.shape["gx"], mesh.shape["gy"]
    owners = outer * inner
    tokens, rows = hidden_in.shape
    width, most = key_grad.shape[1], weight_blocks.shape[2]
    model_width = rows * mesh.shape["gz"]
    flat_rows = height * per_row
    group = -(-rows * per_row // outer)
    pad = -(-max(
        i * group + min(j * most, group) - windows[i * inner + j] * per_row
        for i in range(outer) for j in range(inner)) // 8) * 8
    dims = (outer, inner, model_width, most, per_row, height, pad)
    f32, bf16 = jnp.float32, jnp.bfloat16
    vmem, dma = pltpu.VMEM, pltpu.SemaphoreType.DMA
    in_vmem = pl.BlockSpec(memory_space=pltpu.VMEM)
    in_hbm = pl.BlockSpec(memory_space=pltpu.HBM)
    hgrad, wgrad = pl.pallas_call(
        functools.partial(fast_kernel, dims, windows),
        out_shape=(jax.ShapeDtypeStruct((tokens, rows), bf16), jax.ShapeDtypeStruct((most, LANE), f32)),
        in_specs=[pl.BlockSpec(memory_space=pltpu.SMEM), in_hbm, in_vmem] + [in_hbm] * 3,
        out_specs=(in_vmem, in_vmem),
        scratch_shapes=[
            vmem((tokens, rows), bf16), vmem((tokens, rows), bf16), vmem((most, LANE), bf16),
            vmem((outer, 2, 2, 2, tokens // 2, width), bf16),
            vmem((owners, height, tokens), bf16), vmem((owners, height, tokens), bf16),
            vmem((owners, height, tokens), bf16), vmem((owners, height, tokens), bf16),
            vmem((rows, tokens), f32),
            vmem((pad + max(flat_rows, most), LANE), f32), vmem((flat_rows, LANE), f32),
            vmem((height, width), bf16), vmem((height, width), f32), vmem((flat_rows + most, LANE), f32),
            vmem((8, LANE), f32), vmem((8, LANE), f32), vmem((8, LANE), f32), vmem((8, LANE), f32),
            dma((5,)),
        ] + [dma((outer,))] * 8 + [dma((owners,))] * 4 + [dma((2,))] * 2,
        compiler_params=pltpu.CompilerParams(
            collective_id=0, has_side_effects=True),
    )(block_count, hidden_in, norm_gain.reshape(1, rows), normed_grad, key_grad,
      weight_blocks.reshape(most, LANE))
    return hgrad, wgrad.reshape(1, 1, most, LANE)


def block_layout(counts, blocks, owners, most):
    ends = jnp.cumsum(counts)
    starts = ends - counts
    block_ids = jnp.arange(blocks, dtype=jnp.int32)
    owner = jnp.searchsorted(ends, block_ids, side="right")
    gather_index = owner * most + block_ids - starts[owner]
    slot_owner = jnp.arange(owners * most, dtype=jnp.int32) // most
    slot_within = jnp.arange(owners * most, dtype=jnp.int32) % most
    valid = slot_within < counts[slot_owner]
    source = jnp.clip(starts[slot_owner] + slot_within, 0, blocks - 1)
    return (gather_index, source, valid)


def select_rows(index, keep, rows):
    columns = jnp.arange(rows.shape[0], dtype=jnp.int32)
    onehot = (index[:, None] == columns[None, :]) & keep[:, None]
    if rows.dtype == jnp.bfloat16:
        picked = jnp.dot(onehot.astype(jnp.bfloat16), rows, preferred_element_type=jnp.float32)
        return picked.astype(jnp.bfloat16)
    return jnp.dot(
        onehot.astype(jnp.float32),
        rows,
        precision=lax.Precision.HIGHEST,
        preferred_element_type=jnp.float32,
    )


def select_groups(index, keep, rows):

    def one_group(items):
        return select_rows(items[0], items[1], items[2])

    return lax.map(one_group, (index, keep, rows))


def shards(hidden_in, norm_gain, normed_grad, key_grad, weight_blocks, block_count):
    outer_size = lax.axis_size("gx")
    inner_size = lax.axis_size("gy")
    owners = outer_size * inner_size
    most = weight_blocks.shape[2]
    group_slots_count = inner_size * most
    group_rows = hidden_in.shape[1]
    width = key_grad.shape[1]
    blocks = group_rows * width // 128
    group_blocks = (blocks + outer_size - 1) // outer_size
    model_width = group_rows * lax.axis_size("gz")
    gather_index, source, valid = block_layout(block_count[0], blocks, owners, most)
    outer_index = lax.axis_index("gx")
    padded_index = jnp.pad(gather_index, (0, outer_size * group_blocks - blocks), mode="edge")
    group_offsets = jnp.arange(outer_size, dtype=jnp.int32)[:, None]
    local_index = jnp.clip(
        padded_index.reshape(outer_size, group_blocks) - group_offsets * group_slots_count,
        0,
        group_slots_count - 1,
    )
    local_source = jnp.clip(
        source.reshape(outer_size, group_slots_count) - group_offsets * group_blocks,
        0,
        group_blocks - 1,
    )
    local_valid = valid.reshape(outer_size, group_slots_count)
    all_rows = jnp.ones((outer_size, group_blocks), dtype=bool)
    local_blocks = weight_blocks.reshape(most, 128)
    gathered = lax.all_gather(local_blocks, ("gx", "gy"), axis=0, tiled=True)
    dense = select_groups(
        local_index, all_rows, gathered.reshape(outer_size, group_slots_count, 128)
    )
    weight = dense.reshape(outer_size * group_blocks, 128)[:blocks].reshape(group_rows, width)
    hfloat = hidden_in.astype(jnp.float32)
    squares = lax.psum(jnp.sum(hfloat * hfloat, axis=1), "gz")
    rstd = lax.rsqrt(squares / model_width + EPS)
    normed = (hfloat * rstd[:, None] * norm_gain).astype(jnp.bfloat16)
    dnorm = normed_grad.astype(jnp.float32) + lax.dot_general(
        key_grad, weight, (((1,), (1,)), ((), ())), preferred_element_type=jnp.float32
    )
    proj = lax.psum(jnp.sum(norm_gain * dnorm * hfloat, axis=1), "gz")
    grad = norm_gain * dnorm * rstd[:, None] - hfloat * (rstd**3 * proj / model_width)[:, None]
    hidden_grad = grad.astype(jnp.bfloat16)
    dweight = lax.dot_general(
        normed, key_grad, (((0,), (0,)), ((), ())), preferred_element_type=jnp.float32
    )
    flat = dweight.reshape(blocks, 128)
    flat_padded = jnp.pad(flat, ((0, outer_size * group_blocks - blocks), (0, 0)))
    group_sum = lax.psum_scatter(flat_padded, "gx", scatter_dimension=0, tiled=True)
    slot_source = lax.dynamic_index_in_dim(local_source, outer_index, 0, keepdims=False)
    slot_valid = lax.dynamic_index_in_dim(local_valid, outer_index, 0, keepdims=False)
    slotted = select_rows(slot_source, slot_valid, group_sum)
    owned = lax.psum_scatter(slotted, "gy", scatter_dimension=0, tiled=True)
    return (hidden_grad, owned.reshape(1, 1, most, 128))


def solution(mesh):
    placed = (
        P(("gx", "gy"), "gz"),
        P("gz"),
        P(("gx", "gy"), "gz"),
        P(("gx", "gy"), None),
        P(("gx", "gy"), "gz", None, None),
        P("gz", None),
    )

    def body(*args):
        plan = fast_plan(mesh, args[0], args[3], args[4])
        if plan is None:
            return shards(*args)
        return fast_shards(mesh, plan, *args)

    return jax.shard_map(
        body,
        mesh=mesh,
        in_specs=placed,
        out_specs=(P(("gx", "gy"), "gz"), P(("gx", "gy"), "gz", None, None)),
        check_vma=False,
    )
```

profile of v0, /device:TPU:26, one launch (start us, length us, event | category | flops | bytes accessed | tf_op | source)
XLA Modules:
  0.0 45.9 jit_solution(6976941185520543426)
XLA Ops:
  0.6 42.7 %shard_map.77 = (bf16[128,2048]{1,0:T(8,128)(2,1)}, f32[520,128]{1,0:T(8,128)}) custom-call(s32[1,16]{1,0:T(1,128)} %count_ref.1, bf16[128,2048]{1,0:T(8,128)(2,1)} %hidden_hbm.1, f32[1,2048]{1,0:T(1,128)} %bitcast.5, bf16[128,2048]{1,0:T(8,128)(2,1)} %ngrad_hbm.1, bf16[128,512]{1,0:T(8,128)(2,1)} %key_hbm.1, bf16[520,128]{1,0:T(8,128)(2,1)} %bitcast.4), custom_call_target="tpu_custom_call" | custom-call | tf_op jit(solution)/shard_map/pallas_call | solution.py:253
  43.3 0.0 copy-start
  43.3 1.9 %copy.10 = bf16[128,2048]{1,0:T(8,128)(2,1)} copy(bf16[128,2048]{1,0:T(8,128)(2,1)} %get-tuple-element.8) | data formatting | bytes 1048576
  45.2 0.0 copy-done
  45.2 0.7 %copy.11 = f32[1,1,520,128]{3,2,1,0:T(8,128)} copy(f32[1,1,520,128]{3,2,1,0:T(8,128)S(1)} %bitcast.3) | data formatting | bytes 532480
Async XLA Ops:
  43.3 1.9 %copy-start = (f32[520,128]{1,0:T(8,128)S(1)}, f32[520,128]{1,0:T(8,128)}, u32[]{:S(2)}) copy-start(f32[520,128]{1,0:T(8,128)} %get-tuple-element.5) | copy-start | bytes 798724
where the time goes:
time: 46.2 us; the launch traced here: 45.9 us
  Pallas kernels  42.7 us (92%)
  local copies, waits for them, and re-layouts  2.63 us (6%)
  between operations  0.65 us (1%)
    pallas_call x1, Pallas kernels, fast_shards(): pl.pallas_call(functools.partial(fast_kernel, dims, windows), out_shape=(...  42.7 us
    unnamed x4, local copies, waits for them, and re-layouts  2.63 us

commit v1 on v0

v1 whole, which is shorter than its diff:
```python
import functools
import jax
import jax.numpy as jnp
from jax import lax
from jax.experimental import pallas as pl
from jax.experimental.pallas import tpu as pltpu
from jax.sharding import PartitionSpec as P

EPS = 1e-06
LANE = 128
MESH = pl.DeviceIdType.MESH
VMEM_BUDGET = 48 * 2**20


def owner_windows(group, inner, most, per_row, rows):
    lows, highs = [], []
    for j in range(inner):
        low = max(j, group - (inner - j) * most)
        high = min(min(j * most, group - (inner - j)) + most, group)
        lows.append(low // per_row // 8 * 8)
        highs.append(-(-high // per_row))
    height = -(-max(h - l for l, h in zip(lows, highs)) // 16) * 16
    return [min(low, rows - height) for low in lows], height


def sum_orders(outer):
    table = []
    for a in range(outer):
        up, down = list(range(outer - 1, a, -1)), list(range(a))
        table.append((up + down if len(up) >= len(down) else down + up) + [a])
    return table


def gather_orders(outer):
    table = []
    for a in range(outer):
        row = [a]
        for s in range(1, outer):
            row += [p for p in (a - s, a + s) if 0 <= p < outer]
        table.append(row)
    return table


def fast_kernel(
    dims, lows,
    count_ref, hidden_hbm, gain_ref, ngrad_hbm, key_hbm, wb_hbm,
    hgrad_ref, wgrad_ref,
    hidden_ref, ngrad_ref, wb_ref, kall, wwin, h_send, h_recv, p_send, p_recv,
    feat, grow, gcol, wpad, wflat, dacc, rs_send, rs_recv, dflat,
    sq_send, sq_recv, rrow, pj_acc, pj_recv, py_send, py_recv,
    own_sem, k_ssem, k_rsem, up_ssem, dn_ssem, w_rsem, h_ssem, h_rsem, p_ssem, p_rsem,
    rs_ssem, rs_rsem, r_ssem, r_rsem, pj_ssem, pj_rsem, y_ssem, y_rsem,
):
    outer, inner, model_width, most, per_row, height, pad = dims
    f32, bf16 = jnp.float32, jnp.bfloat16
    a, b, g = lax.axis_index("gx"), lax.axis_index("gy"), lax.axis_index("gz")
    x, c = b // 2, b % 2
    me = a * inner + b
    tokens, rows = hidden_ref.shape
    width = kall.shape[2]
    owners = outer * inner
    span = rows // outer
    chunks = rows // LANE
    last = outer - 1
    low_me = lows[0] + x * (lows[2] - lows[0]) + c * (lows[1] - lows[0]) + x * c * (
        lows[3] - lows[2] - lows[1] + lows[0])
    mid = height // 32 * 16 + (16 if height // 16 % 2 else 0)
    halves = (slice(0, mid), slice(mid, height))
    interior = jnp.logical_and(a > 0, a < last)
    ends = jnp.logical_or(a == 0, a == last)

    def pick(table, k):
        value = jnp.int32(0)
        for j in range(outer):
            value = value + jnp.where(a == j, table[j][k], 0)
        return value

    sum_table, gather_table = sum_orders(outer), gather_orders(outer)

    def peer(k):
        px = 1 - x if k // 2 else x
        pc = 1 - c if k % 2 else c
        return px * 2 + pc

    def slot_of(j):
        return (x if j // 2 == 0 else 1 - x) * 2 + (c if j % 2 == 0 else 1 - c)

    def remote(src, dst, send, recv, gx, gy, gz):
        return pltpu.make_async_remote_copy(
            src_ref=src, dst_ref=dst, send_sem=send, recv_sem=recv,
            device_id=(gx, gy, gz), device_id_type=MESH)

    sends = []

    def start(copy):
        copy.start()
        sends.append((copy, None))
        return copy

    def start_if(cond, copy):
        pl.when(cond)(copy.start)
        sends.append((copy, cond))
        return copy

    own = [
        pltpu.make_async_copy(wb_hbm, wb_ref, own_sem.at[0]),
        pltpu.make_async_copy(hidden_hbm, hidden_ref, own_sem.at[1]),
        pltpu.make_async_copy(key_hbm, kall.at[0], own_sem.at[2]),
        pltpu.make_async_copy(ngrad_hbm, ngrad_ref, own_sem.at[3]),
    ]
    for copy in own:
        copy.start()
    barrier = pltpu.get_barrier_semaphore()
    for k in range(1, inner):
        pl.semaphore_signal(barrier, inc=1, device_id=(a, peer(k), g), device_id_type=MESH)
    pl.semaphore_signal(barrier, inc=1, device_id=(a, b, 1 - g), device_id_type=MESH)

    @pl.when(a < last)
    def _():
        pl.semaphore_signal(barrier, inc=1, device_id=(a + 1, b, g), device_id_type=MESH)

    @pl.when(a > 0)
    def _():
        pl.semaphore_signal(barrier, inc=1, device_id=(a - 1, b, g), device_id_type=MESH)

    begin = jnp.int32(0)
    count = jnp.int32(0)
    for o in range(owners):
        value = count_ref[0, o]
        begin = begin + jnp.where(o < me, value, 0)
        count = count + jnp.where(me == o, value, 0)
    offset = jnp.clip(begin - (a * span + low_me) * per_row, 0, pad)
    flat_rows = height * per_row
    slot = lax.broadcasted_iota(jnp.int32, (most, LANE), 0)
    wpad[...] = jnp.zeros_like(wpad)
    own[0].wait()
    wpad[pad:pad + most, :] = jnp.where(slot < count, wb_ref[...].astype(f32), 0.0)
    wflat[...] = wpad[pl.ds(pad - offset, flat_rows), :]
    for i in range(per_row):
        wwin[a, :, i * LANE:(i + 1) * LANE] = wflat[pl.ds(i, height, stride=per_row), :].astype(bf16)

    own[1].wait()
    squares = jnp.zeros((tokens, LANE), f32)
    for i in range(chunks):
        part = hidden_ref[:, i * LANE:(i + 1) * LANE].astype(f32)
        squares = squares + part * part
    row_sum = jnp.sum(squares, axis=1, keepdims=True)
    sq_send[...] = jnp.broadcast_to(row_sum, (tokens, LANE)).T[0:8, :]

    own[2].wait()
    pl.semaphore_wait(barrier, inner + jnp.where(a < last, 1, 0) + jnp.where(a > 0, 1, 0))

    sq_copy = start(remote(sq_send, sq_recv, y_ssem.at[0], y_rsem.at[0], a, b, 1 - g))
    k_copy = {k: start(remote(kall.at[0], kall.at[k], k_ssem.at[k], k_rsem.at[k], a, peer(k), g))
              for k in (2, 1)}

    def gather(piece, h, up):
        part = wwin.at[piece, halves[h]]
        send = (up_ssem if up else dn_ssem).at[piece, h]
        return remote(part, part, send, w_rsem.at[piece, h], a + 1 if up else a - 1, b, g)

    for h in range(2):
        start_if(a < last, gather(a, h, True))
        start_if(a > 0, gather(a, h, False))

    h_copy, r_copy = {}, {}
    for i in range(outer):
        z = pick(sum_table, i)
        for q in range(span // LANE):
            cols = pl.ds(pl.multiple_of(z * span + q * LANE, LANE), LANE)
            feat[q * LANE:(q + 1) * LANE, :] = hidden_ref[:, cols].astype(f32).T
        for j in range(inner):
            h_send[z, j] = feat[lows[j]:lows[j] + height, :].astype(bf16)
        for k in (2, 3, 1):
            h_copy[i, k] = start(remote(
                h_send.at[z, peer(k)], h_recv.at[z, k], h_ssem.at[z, k], h_rsem.at[z, k], a, peer(k), g))
        if i == 0:
            sq_copy.wait_recv()
            rrow[0] = lax.rsqrt((sq_send[...] + sq_recv[...]) / model_width + EPS)
            for k in (2, 3, 1):
                r_copy[k] = start(remote(
                    rrow.at[0], rrow.at[k], r_ssem.at[k], r_rsem.at[k], a, peer(k), g))

    rstd = jnp.broadcast_to(rrow[0, 0:1, :], (tokens, LANE)).T[:, 0:1]
    for i in range(chunks):
        cols = slice(i * LANE, (i + 1) * LANE)
        gcol[cols, :] = jnp.broadcast_to(gain_ref[:, cols], (LANE, LANE)).T
    own[3].wait()
    local = jnp.zeros((tokens, LANE), f32)
    for i in range(chunks):
        cols = slice(i * LANE, (i + 1) * LANE)
        local = local + gain_ref[:, cols] * ngrad_ref[:, cols].astype(f32) * hidden_ref[:, cols].astype(f32)
    local_sum = jnp.sum(local, axis=1, keepdims=True)
    py_send[...] = jnp.broadcast_to(local_sum, (tokens, LANE)).T[0:8, :]

    k_copy[2].wait_recv()
    k_copy[3] = start(remote(kall.at[2], kall.at[3], k_ssem.at[3], k_rsem.at[3], a, peer(1), g))

    def gather_step(s):
        below, above = a - s >= 0, a + s <= last
        for h in range(2):
            @pl.when(below)
            def _():
                gather(a - s, h, True).wait_recv()
            start_if(jnp.logical_and(below, a < last), gather(a - s, h, True))

            @pl.when(above)
            def _():
                gather(a + s, h, False).wait_recv()
            start_if(jnp.logical_and(above, a > 0), gather(a + s, h, False))

    def keys():
        return kall[...].reshape(inner * tokens, width)

    def p_copy(z, k):
        return remote(p_send.at[z, k], p_recv.at[z, k], p_ssem.at[z, k], p_rsem.at[z, k], a, peer(k), g)

    def project(z):
        product = lax.dot_general(
            wwin[z], keys(), (((1,), (1,)), ((), ())), preferred_element_type=f32)
        p_recv[z, 0] = product[:, 0:tokens].astype(bf16)
        for k in (2, 3, 1):
            p_send[z, k] = product[:, k * tokens:(k + 1) * tokens].astype(bf16)
            p_copy(z, k).start()

    def gain_rows(z):
        return gcol[pl.ds(pl.multiple_of(z * span + low_me, 8), height), :]

    def hidden_rows(z, k):
        return (h_send[z, b] if k == 0 else h_recv[z, k]).astype(f32)

    def partial(i):
        z = pick(sum_table, i)
        gains = gain_rows(z)
        for k in range(1, inner):
            h_copy[i, k].wait_recv()
        normed = [(hidden_rows(z, k) * rrow[k, 0:1, :] * gains).astype(bf16) for k in range(inner)]
        dacc[i] = jnp.dot(jnp.concatenate(normed, axis=1), keys(), preferred_element_type=f32)

    def sum_copy(i, h):
        z = pick(sum_table, i)
        up = (z > a).astype(jnp.int32)
        place = z + (1 - up) * outer
        return remote(rs_send.at[i, halves[h]], rs_recv.at[place, halves[h]],
                      rs_ssem.at[i, h], rs_rsem.at[place, h], a + 2 * up - 1, b, g)

    def sum_send(i, h):
        rs_send[i, halves[h]] = dacc[i, halves[h]].astype(bf16)
        sum_copy(i, h).start()

    def sum_ends(i):
        @pl.when(ends)
        def _():
            for h in range(2):
                sum_send(i, h)

    def sum_wait(place, h):
        part = rs_recv.at[place, halves[h]]
        remote(part, part, rs_ssem.at[0, h], rs_rsem.at[place, h], a, b, 1 - g).wait_recv()

    def sum_interior(i):
        @pl.when(interior)
        def _():
            z = pick(sum_table, i)
            place = z + jnp.where(z > a, 0, outer)
            for h in range(2):
                sum_wait(place, h)
                dacc[i, halves[h]] += rs_recv[place, halves[h]].astype(f32)
                sum_send(i, h)

    def inner_products(z, first):
        gains = gain_rows(z)
        for k in range(inner):
            part = (p_recv[z, 0] if k == 0 else p_send[z, k]).astype(f32)
            term = part * hidden_rows(z, k) * gains
            term = jnp.sum(term.reshape(height // 8, 8, LANE), axis=0)
            pj_acc[k] = term if first else pj_acc[k] + term

    def accumulate(i):
        z = pick(gather_table, i)
        for k in range(1, inner):
            p_copy(z, k).wait_recv()
        feat[...] = jnp.zeros_like(feat)
        for j in range(inner):
            feat[lows[j]:lows[j] + height, :] += p_recv[z, slot_of(j)].astype(f32)
        for q in range(span // LANE):
            cols = pl.ds(pl.multiple_of(z * span + q * LANE, LANE), LANE)
            dnorm = ngrad_ref[:, cols].astype(f32) + feat[q * LANE:(q + 1) * LANE, :].T
            grow[:, cols] = gain_ref[:, cols] * dnorm * rstd

    def project_step(s):
        for piece, there in ((a - s, a - s >= 0), (a + s, a + s <= last)):
            @pl.when(there)
            def _():
                project(piece)

    gather_step(1)
    k_copy[1].wait_recv()
    k_copy[3].wait_recv()
    project(a)
    for k in range(1, inner):
        r_copy[k].wait_recv()
    partial(0)
    sum_ends(0)
    project_step(1)
    partial(1)
    sum_ends(1)
    for s in range(2, last):
        gather_step(s)
        project_step(s)
    for i in range(2, last):
        partial(i)
        sum_ends(i)
    partial(last)
    inner_products(a, True)
    sum_interior(0)
    gather_step(last)
    project_step(last)
    for i in range(1, outer):
        inner_products(pick(gather_table, i), False)
    pj_copy = {k: start(remote(pj_acc.at[k], pj_recv.at[k], pj_ssem.at[k], pj_rsem.at[k], a, peer(k), g))
               for k in (2, 3, 1)}
    accumulate(0)
    for i in range(1, last):
        sum_interior(i)
        accumulate(i)
    for k in range(1, inner):
        pj_copy[k].wait_recv()
    first_row = lax.broadcasted_iota(jnp.int32, (8, LANE), 0) == 0
    py_send[...] = (jnp.where(first_row, py_send[...], 0.0) + pj_acc[0]
                    + pj_recv[1] + pj_recv[2] + pj_recv[3])
    py_copy = start(remote(py_send, py_recv, y_ssem.at[1], y_rsem.at[1], a, b, 1 - g))
    accumulate(last)
    py_copy.wait_recv()
    proj_row = jnp.sum(py_send[...] + py_recv[...], axis=0, keepdims=True)
    proj_all = jnp.broadcast_to(proj_row, (tokens, LANE)).T[:, 0:1]
    scale = rstd * rstd * rstd * proj_all / model_width
    for i in range(chunks):
        cols = slice(i * LANE, (i + 1) * LANE)
        hgrad_ref[:, cols] = (grow[:, cols] - hidden_ref[:, cols].astype(f32) * scale).astype(bf16)

    for h in range(2):
        @pl.when(a > 0)
        def _():
            sum_wait(a, h)
            dacc[last, halves[h]] += rs_recv[a, halves[h]].astype(f32)

        @pl.when(a < last)
        def _():
            sum_wait(a + outer, h)
            dacc[last, halves[h]] += rs_recv[a + outer, halves[h]].astype(f32)
    for i in range(per_row):
        dflat[pl.ds(i, height, stride=per_row), :] = dacc[last, :, i * LANE:(i + 1) * LANE]
    dflat[flat_rows:, :] = jnp.zeros((most, LANE), f32)
    wgrad_ref[...] = jnp.where(slot < count, dflat[pl.ds(offset, most), :], 0.0)

    for copy, cond in sends:
        if cond is None:
            copy.wait_send()
        else:
            pl.when(cond)(copy.wait_send)
    for z in range(outer):
        for k in range(1, inner):
            p_copy(z, k).wait_send()
    for i in range(last):
        for h in range(2):
            sum_copy(i, h).wait_send()


def fast_plan(mesh, hidden, key, wb):
    outer, inner, halves = (mesh.shape[n] for n in ("gx", "gy", "gz"))
    tokens, rows, width, most = hidden.shape[0], hidden.shape[1], key.shape[1], wb.shape[2]
    if inner != 4 or halves != 2 or outer < 3 or tokens != LANE or width % LANE or most % 8:
        return None
    per_row = width // LANE
    if rows % (outer * LANE):
        return None
    span = rows // outer
    lows, height = owner_windows(span * per_row, inner, most, per_row, span)
    if height < 32 or min(lows) < 0:
        return None
    held = 4 * owners_bytes(outer, inner, height, tokens) + 4 * outer * height * width * 4 + 8 * tokens * rows * 4
    if held > VMEM_BUDGET:
        return None
    return lows, height, per_row


def owners_bytes(outer, inner, height, tokens):
    return outer * inner * height * tokens * 2


def fast_shards(mesh, plan, hidden_in, norm_gain, normed_grad, key_grad, weight_blocks, block_count):
    lows, height, per_row = plan
    outer, inner = mesh.shape["gx"], mesh.shape["gy"]
    tokens, rows = hidden_in.shape
    width, most = key_grad.shape[1], weight_blocks.shape[2]
    model_width = rows * mesh.shape["gz"]
    flat_rows = height * per_row
    span = rows // outer
    pad = -(-max(min(j * most, span * per_row) - lows[j] * per_row for j in range(inner)) // 8) * 8
    dims = (outer, inner, model_width, most, per_row, height, pad)
    f32, bf16 = jnp.float32, jnp.bfloat16
    vmem, dma = pltpu.VMEM, pltpu.SemaphoreType.DMA
    in_vmem = pl.BlockSpec(memory_space=pltpu.VMEM)
    in_hbm = pl.BlockSpec(memory_space=pltpu.HBM)
    pieces = vmem((outer, inner, height, tokens), bf16)
    small = vmem((8, LANE), f32)
    smalls = vmem((inner, 8, LANE), f32)
    hgrad, wgrad = pl.pallas_call(
        functools.partial(fast_kernel, dims, lows),
        out_shape=(jax.ShapeDtypeStruct((tokens, rows), bf16), jax.ShapeDtypeStruct((most, LANE), f32)),
        in_specs=[pl.BlockSpec(memory_space=pltpu.SMEM), in_hbm, in_vmem] + [in_hbm] * 3,
        out_specs=(in_vmem, in_vmem),
        scratch_shapes=[
            vmem((tokens, rows), bf16), vmem((tokens, rows), bf16), vmem((most, LANE), bf16),
            vmem((inner, tokens, width), bf16), vmem((outer, height, width), bf16),
            pieces, pieces, pieces, pieces,
            vmem((span, tokens), f32), vmem((tokens, rows), f32), vmem((rows, LANE), f32),
            vmem((pad + max(flat_rows, most), LANE), f32), vmem((flat_rows, LANE), f32),
            vmem((outer, height, width), f32), vmem((outer, height, width), bf16),
            vmem((2 * outer, height, width), bf16), vmem((flat_rows + most, LANE), f32),
            small, small, smalls, smalls, smalls, small, small,
            dma((4,)), dma((inner,)), dma((inner,)),
            dma((outer, 2)), dma((outer, 2)), dma((outer, 2)),
            dma((outer, inner)), dma((outer, inner)), dma((outer, inner)), dma((outer, inner)),
            dma((outer, 2)), dma((2 * outer, 2)),
            dma((inner,)), dma((inner,)), dma((inner,)), dma((inner,)), dma((2,)), dma((2,)),
        ],
        compiler_params=pltpu.CompilerParams(
            collective_id=0, has_side_effects=True),
    )(block_count, hidden_in, norm_gain.reshape(1, rows), normed_grad, key_grad,
      weight_blocks.reshape(most, LANE))
    return hgrad, wgrad.reshape(1, 1, most, LANE)


def block_layout(counts, blocks, owners, most):
    ends = jnp.cumsum(counts)
    starts = ends - counts
    block_ids = jnp.arange(blocks, dtype=jnp.int32)
    owner = jnp.searchsorted(ends, block_ids, side="right")
    gather_index = owner * most + block_ids - starts[owner]
    slot_owner = jnp.arange(owners * most, dtype=jnp.int32) // most
    slot_within = jnp.arange(owners * most, dtype=jnp.int32) % most
    valid = slot_within < counts[slot_owner]
    source = jnp.clip(starts[slot_owner] + slot_within, 0, blocks - 1)
    return (gather_index, source, valid)


def select_rows(index, keep, rows):
    columns = jnp.arange(rows.shape[0], dtype=jnp.int32)
    onehot = (index[:, None] == columns[None, :]) & keep[:, None]
    if rows.dtype == jnp.bfloat16:
        picked = jnp.dot(onehot.astype(jnp.bfloat16), rows, preferred_element_type=jnp.float32)
        return picked.astype(jnp.bfloat16)
    return jnp.dot(
        onehot.astype(jnp.float32),
        rows,
        precision=lax.Precision.HIGHEST,
        preferred_element_type=jnp.float32,
    )


def select_groups(index, keep, rows):

    def one_group(items):
        return select_rows(items[0], items[1], items[2])

    return lax.map(one_group, (index, keep, rows))


def shards(hidden_in, norm_gain, normed_grad, key_grad, weight_blocks, block_count):
    outer_size = lax.axis_size("gx")
    inner_size = lax.axis_size("gy")
    owners = outer_size * inner_size
    most = weight_blocks.shape[2]
    group_slots_count = inner_size * most
    group_rows = hidden_in.shape[1]
    width = key_grad.shape[1]
    blocks = group_rows * width // 128
    group_blocks = (blocks + outer_size - 1) // outer_size
    model_width = group_rows * lax.axis_size("gz")
    gather_index, source, valid = block_layout(block_count[0], blocks, owners, most)
    outer_index = lax.axis_index("gx")
    padded_index = jnp.pad(gather_index, (0, outer_size * group_blocks - blocks), mode="edge")
    group_offsets = jnp.arange(outer_size, dtype=jnp.int32)[:, None]
    local_index = jnp.clip(
        padded_index.reshape(outer_size, group_blocks) - group_offsets * group_slots_count,
        0,
        group_slots_count - 1,
    )
    local_source = jnp.clip(
        source.reshape(outer_size, group_slots_count) - group_offsets * group_blocks,
        0,
        group_blocks - 1,
    )
    local_valid = valid.reshape(outer_size, group_slots_count)
    all_rows = jnp.ones((outer_size, group_blocks), dtype=bool)
    local_blocks = weight_blocks.reshape(most, 128)
    gathered = lax.all_gather(local_blocks, ("gx", "gy"), axis=0, tiled=True)
    dense = select_groups(
        local_index, all_rows, gathered.reshape(outer_size, group_slots_count, 128)
    )
    weight = dense.reshape(outer_size * group_blocks, 128)[:blocks].reshape(group_rows, width)
    hfloat = hidden_in.astype(jnp.float32)
    squares = lax.psum(jnp.sum(hfloat * hfloat, axis=1), "gz")
    rstd = lax.rsqrt(squares / model_width + EPS)
    normed = (hfloat * rstd[:, None] * norm_gain).astype(jnp.bfloat16)
    dnorm = normed_grad.astype(jnp.float32) + lax.dot_general(
        key_grad, weight, (((1,), (1,)), ((), ())), preferred_element_type=jnp.float32
    )
    proj = lax.psum(jnp.sum(norm_gain * dnorm * hfloat, axis=1), "gz")
    grad = norm_gain * dnorm * rstd[:, None] - hfloat * (rstd**3 * proj / model_width)[:, None]
    hidden_grad = grad.astype(jnp.bfloat16)
    dweight = lax.dot_general(
        normed, key_grad, (((0,), (0,)), ((), ())), preferred_element_type=jnp.float32
    )
    flat = dweight.reshape(blocks, 128)
    flat_padded = jnp.pad(flat, ((0, outer_size * group_blocks - blocks), (0, 0)))
    group_sum = lax.psum_scatter(flat_padded, "gx", scatter_dimension=0, tiled=True)
    slot_source = lax.dynamic_index_in_dim(local_source, outer_index, 0, keepdims=False)
    slot_valid = lax.dynamic_index_in_dim(local_valid, outer_index, 0, keepdims=False)
    slotted = select_rows(slot_source, slot_valid, group_sum)
    owned = lax.psum_scatter(slotted, "gy", scatter_dimension=0, tiled=True)
    return (hidden_grad, owned.reshape(1, 1, most, 128))


def solution(mesh):
    placed = (
        P(("gx", "gy"), "gz"),
        P("gz"),
        P(("gx", "gy"), "gz"),
        P(("gx", "gy"), None),
        P(("gx", "gy"), "gz", None, None),
        P("gz", None),
    )

    def body(*args):
        plan = fast_plan(mesh, args[0], args[3], args[4])
        if plan is None:
            return shards(*args)
        return fast_shards(mesh, plan, *args)

    return jax.shard_map(
        body,
        mesh=mesh,
        in_specs=placed,
        out_specs=(P(("gx", "gy"), "gz"), P(("gx", "gy"), "gz", None, None)),
        check_vma=False,
    )
```

time: 46.2 us -> 32.4 us (0.70)
  the two profiles are of different devices: /device:TPU:26 before, /device:TPU:0 now
where the time goes in v1:
time: 32.4 us; the launch traced here: 32.1 us
  Pallas kernels  28.9 us (89%)
  local copies, waits for them, and re-layouts  2.63 us (8%)
  between operations  0.65 us (2%)
    pallas_call x1, Pallas kernels, fast_shards(): pl.pallas_call(functools.partial(fast_kernel, dims, lows), out_shape=(jax...  28.9 us
    unnamed x4, local copies, waits for them, and re-layouts  2.63 us

profile of v1, /device:TPU:0, one launch (start us, length us, event | category | flops | bytes accessed | tf_op | source)
XLA Modules:
  0.0 32.1 jit_solution(9489701144230442372)
XLA Ops:
  0.6 28.9 %shard_map.77 = (bf16[128,2048]{1,0:T(8,128)(2,1)}, f32[520,128]{1,0:T(8,128)}) custom-call(s32[1,16]{1,0:T(1,128)} %count_ref.1, bf16[128,2048]{1,0:T(8,128)(2,1)} %hidden_hbm.1, f32[1,2048]{1,0:T(1,128)} %bitcast.5, bf16[128,2048]{1,0:T(8,128)(2,1)} %ngrad_hbm.1, bf16[128,512]{1,0:T(8,128)(2,1)} %key_hbm.1, bf16[520,128]{1,0:T(8,128)(2,1)} %bitcast.4), custom_call_target="tpu_custom_call" | custom-call | tf_op jit(solution)/shard_map/pallas_call | solution.py:409
  29.5 0.0 copy-start
  29.5 1.9 %copy.10 = bf16[128,2048]{1,0:T(8,128)(2,1)} copy(bf16[128,2048]{1,0:T(8,128)(2,1)} %get-tuple-element.8) | data formatting | bytes 1048576
  31.4 0.0 copy-done
  31.4 0.7 %copy.11 = f32[1,1,520,128]{3,2,1,0:T(8,128)} copy(f32[1,1,520,128]{3,2,1,0:T(8,128)S(1)} %bitcast.3) | data formatting | bytes 532480
Async XLA Ops:
  29.5 1.9 %copy-start = (f32[520,128]{1,0:T(8,128)S(1)}, f32[520,128]{1,0:T(8,128)}, u32[]{:S(2)}) copy-start(f32[520,128]{1,0:T(8,128)} %get-tuple-element.5) | copy-start | bytes 798724
